TPU v7x, 8 devices: a whole 2x2x1 slice. The times are simulated.
8 devices in a mesh: dp: 1 (over z), tp: 2 (over y), ep: 4 (over x, core).
Axes of the slice: x: 2, y: 2, z: 1, core: 2. Of those that a mesh axis runs over, the one named last changes fastest.
Arguments:
- tokens_x: bfloat16 [3072, 2048], P(('dp', 'ep', 'tp'))
- expert_ids: int32 [3072, 8], P(('dp', 'ep', 'tp'))
- route_gate: float32 [3072, 8], P(('dp', 'ep', 'tp'))
- w_gate: bfloat16 [64, 2048, 1024], P('ep', None, 'tp')
- w_up: bfloat16 [64, 2048, 1024], P('ep', None, 'tp')
- w_down: bfloat16 [64, 1024, 2048], P('ep', 'tp')
Outputs:
- output: bfloat16 [3072, 2048], P(('dp', 'ep', 'tp'))
All inputs are finite; a program needn't handle non-finite values.
Results may differ from a plain program's by a relative error of at most 0.00121.
Values are sent between devices in bfloat16 or wider.
A program may use at most 1 GiB of HBM per device.

v0:
```python
import jax
import jax.numpy as jnp
from jax import lax
from jax.sharding import PartitionSpec as P, NamedSharding


def solution(mesh):
    ep_size = mesh.shape['ep']
    row_spec = P(('dp', 'ep', 'tp'), None)
    w_in_spec = P('ep', None, 'tp')
    w_out_spec = P('ep', 'tp', None)

    def local_moe(x_local, ids_local, gate_local, w_gate, w_up, w_down):
        e_local = w_gate.shape[0]
        x_all = lax.all_gather(x_local, ('ep', 'tp'), tiled=True)
        ids_all = lax.all_gather(ids_local, ('ep', 'tp'), tiled=True)
        gate_all = lax.all_gather(gate_local, ('ep', 'tp'), tiled=True)
        num_tok, top_k = ids_all.shape
        local_pairs = num_tok * top_k // ep_size
        expert_cap = local_pairs // e_local
        local_ids = ids_all.reshape(-1) - lax.axis_index('ep') * e_local
        is_local = (local_ids >= 0) & (local_ids < e_local)
        sort_order = jnp.argsort(jnp.where(is_local, local_ids, e_local), stable=True)[:local_pairs]
        tok_rows = sort_order // top_k
        gate_rows = gate_all.reshape(-1)[sort_order]
        x_rows = x_all[tok_rows].reshape(e_local, expert_cap, -1)
        h_gate = jnp.einsum('ecd,edf->ecf', x_rows, w_gate, preferred_element_type=jnp.float32)
        h_up = jnp.einsum('ecd,edf->ecf', x_rows, w_up, preferred_element_type=jnp.float32)
        hidden = (jax.nn.silu(h_gate) * h_up).astype(jnp.bfloat16)
        out_rows = jnp.einsum('ecf,efd->ecd', hidden, w_down, preferred_element_type=jnp.float32)
        out_rows = out_rows.reshape(local_pairs, -1) * gate_rows[:, None]
        partial_sum = jax.ops.segment_sum(out_rows, tok_rows, num_segments=num_tok)
        y_local = lax.psum_scatter(partial_sum, ('ep', 'tp'), scatter_dimension=0, tiled=True)
        return y_local.astype(jnp.bfloat16)

    return jax.shard_map(local_moe, mesh=mesh, in_specs=(row_spec, row_spec, row_spec, w_in_spec, w_in_spec, w_out_spec), out_specs=row_spec, check_vma=False)
```

profile of v0, /device:TPU:0, one launch (start us, length us, event | category | flops | bytes accessed | tf_op | source)
XLA Modules:
  0.0 501.7 jit_solution(16775702374984374036)
XLA Ops:
  6.5 0.0 all-gather.2.cloned.1.call-start
  6.5 0.7 all-gather.2.cloned.1.call-update
  7.3 0.0 reduce-scatter.2.cloned.1.call-start
  7.3 14.2 %all_gather.11 = f32[3072,8]{0,1:T(8,128)S(1)} all-gather(f32[384,8]{0,1:T(8,128)} %param.8), channel_id=1, replica_groups=mesh['dp'=1,'tp'=2,'ep'=4] {'ep','tp'}, dimensions={0}, use_global_device_ids=true | all-gather | bytes 110592 | tf_op jit(solution)/shard_map/all_gather | solution.py:17
  21.5 0.5 copy.8
  22.0 0.8 reshape.15
  22.8 11.8 %all_gather.9 = s32[3072,8]{0,1:T(8,128)S(1)} all-gather(s32[384,8]{0,1:T(8,128)} %param.7), channel_id=1, replica_groups=mesh['dp'=1,'tp'=2,'ep'=4] {'ep','tp'}, dimensions={0}, use_global_device_ids=true | all-gather | bytes 110592 | tf_op jit(solution)/shard_map/all_gather | solution.py:16
  34.6 0.5 copy.7
  35.1 0.8 sub.17
  35.9 11.3 %sort.17 = (s32[24576]{0:T(1024)}, s32[24576]{0:T(1024)S(1)}) sort(s32[24576]{0:T(1024)S(1)} %and_select_fusion, s32[24576]{0:T(1024)S(1)} %iota.4), dimensions={0}, to_apply=%region_0.1 | sort | flops 368640 | bytes 393216 | tf_op jit(solution)/shard_map/jit(argsort)/sort | solution.py:23
  47.2 0.6 fusion.7
  47.8 34.3 %gather_fusion.1 = f32[6144]{0:T(1024)S(1)} fusion(f32[24576]{0:T(1024)S(1)} %reshape.15, s32[6144]{0:T(1024)S(1)} %get-tuple-element.7), kind=kCustom, calls=%fused_computation.1 | custom fusion | bytes 73728 | tf_op jit(solution)/shard_map/gather | solution.py:25
  82.1 0.0 all-gather.2.cloned.1.call-done
  82.1 52.5 %gather_fusion = bf16[6144,2048]{1,0:T(8,128)(2,1)} fusion(bf16[3072,2048]{1,0:T(8,128)(2,1)} %all-gather.2.cloned.1.call-done, s32[6144]{0:T(1024)S(1)} %get-tuple-element.8), kind=kCustom, calls=%fused_computation | custom fusion | bytes 50356224 | tf_op jit(solution)/shard_map/gather | solution.py:26
  134.7 35.6 %fusion.11 = f32[16,384,512]{2,1,0:T(8,128)} fusion(bf16[16,384,2048]{2,1,0:T(8,128)(2,1)} %bitcast.13, bf16[16,2048,512]{2,1,0:T(8,128)(2,1)} %param.9), kind=kOutput, calls=%fused_computation.24 | convolution fusion | flops 12884901888 | bytes 71303168 | tf_op jit(solution)/shard_map/ecd,edf->ecf/dot_general | solution.py:27
  170.3 53.3 %fusion.2 = f32[16,384,2048]{2,1,0:T(8,128)} fusion(bf16[16,512,2048]{2,1,0:T(8,128)(2,1)} %param.11, f32[16,384,512]{2,1,0:T(8,128)} %fusion.11, bf16[16,384,2048]{2,1,0:T(8,128)(2,1)} %bitcast.14, bf16[16,2048,512]{2,1,0:T(8,128)(2,1)} %param.10), kind=kOutput, calls=%fused_computation.7 | convolution fusion | flops 25788678144 | bytes 155189248 | tf_op jit(solution)/shard_map/ecf,efd->ecd/dot_general | solution.py:30
  223.6 34.5 %bitcast_multiply_fusion = f32[6144,2048]{1,0:T(8,128)} fusion(f32[16,384,2048]{2,1,0:T(8,128)} %fusion.2, f32[6144]{0:T(1024)S(1)} %gather_fusion.1), kind=kLoop, calls=%fused_computation.3 | loop fusion | flops 12582912 | bytes 100687872 | tf_op jit(solution)/shard_map/mul | solution.py:31
  258.1 86.8 %scatter_custom_fusion = f32[3072,2048]{1,0:T(8,128)} fusion(s32[6144]{0:T(1024)} %get-tuple-element.9, f32[6144,2048]{1,0:T(8,128)} %bitcast_multiply_fusion, f32[]{:T(128)} %constant.11.clone.1), kind=kCustom, calls=%fused_computation.5 | custom fusion | flops 12582912 | bytes 25166336 | tf_op jit(solution)/shard_map/scatter-add | solution.py:32
  344.9 0.0 reduce-scatter.2.cloned.1.call-update
  344.9 146.6 %reduce-scatter.2.cloned.1.call-done = f32[384,2048]{1,0:T(8,128)} async-done(((f32[3072,2048]{1,0:T(8,128)}), f32[384,2048]{1,0:T(8,128)}) %reduce-scatter.2.cloned.1.call-update) | async-done | bytes 3145744 | tf_op jit(solution)/shard_map/reduce_scatter | solution.py:33
  491.6 3.3 convert_element_type.7
  (3 shorter events, 0.0 us)
Async XLA Ops:
  6.5 75.6 %all-gather.2.cloned.1.call-start = ((), (), s32[]{:S(2)}) async-start(), calls=%async_computation.1 | async-start | bytes 14155776 | tf_op jit(solution)/shard_map/all_gather | solution.py:15
  7.3 484.3 %reduce-scatter.2.cloned.1.call-start = ((), (), s32[]{:S(2)}) async-start(), calls=%async_computation.2 | async-start | bytes 28311552 | tf_op jit(solution)/shard_map/reduce_scatter | solution.py:33
Sparse Core Ops, SparseCore 0:
  9.1 70.0 all-gather.1
  345.1 146.4 reduce-scatter.1
where the time goes:
time: 502 us
  waiting for transfers between devices  147 us (29%)
  other arithmetic  136 us (27%)
  local copies, waits for them, and re-layouts  89.3 us (18%)
  matrix products  89 us (18%)
  blocking collectives  26.1 us (5%)
  between operations  13.5 us (3%)
    reduce_scatter x1, waiting for transfers between devices, local_moe(): lax.psum_scatter(partial_sum, ('ep', 'tp'), scatter_dimension=0, tiled=True)  147 us
    scatter-add x1, other arithmetic, local_moe(): partial_sum = jax.ops.segment_sum(out_rows, tok_rows, num_segments=num_tok)  86.8 us
    dot_general x1, matrix products, local_moe(): jnp.einsum('ecf,efd->ecd', hidden, w_down, preferred_element_type=jnp.flo...  53.3 us
    gather x1, local copies, waits for them, and re-layouts, local_moe(): x_rows = x_all[tok_rows].reshape(e_local, expert_cap, -1)  52.5 us
    dot_general x1, matrix products, local_moe(): jnp.einsum('ecd,edf->ecf', x_rows, w_gate, preferred_element_type=jnp.flo...  35.6 us
    mul x1, other arithmetic, local_moe(): out_rows = out_rows.reshape(local_pairs, -1) * gate_rows[:, None]  34.5 us
    gather x1, local copies, waits for them, and re-layouts, local_moe(): gate_rows = gate_all.reshape(-1)[sort_order]  34.3 us
    all_gather x1, blocking collectives, local_moe(): gate_all = lax.all_gather(gate_local, ('ep', 'tp'), tiled=True)  14.2 us
  transfers between devices with their start and end apart: 2, of which 1 were waited for; matrix products, arithmetic and copies ran while one was open for 10% of the time, Pallas kernels for 0%

commit v1 on v0

v1 whole, which is shorter than its diff:
```python
import functools

import jax
import jax.numpy as jnp
from jax import lax
from jax.experimental import pallas as pl
from jax.experimental.pallas import tpu as pltpu
from jax.sharding import PartitionSpec as P

MESH = pl.DeviceIdType.MESH
ROWS = 384
HALF = 192
CAP = 48
DM = 2048
FF = 512
EL = 16
CH = 256
NCH = DM // CH
UNITS = 2 * NCH
WSLOTS = 3


def moe_kernel(rt_ref, x_hbm, wg_hbm, wu_hbm, wd_hbm, y_hbm,
               xa, rtb, key, dt, gp, utri, xdp, hb, wgv, wuv, wdv, ob,
               pm, ps, dr, rf, rs, yv, yst,
               sem_x, sem_w, sem_wd, sem_rs, sem_rr, sem_os, sem_or,
               sem_as, sem_ar, sem_ds, sem_dr, sem_ps, sem_pr, sem_fs, sem_fr,
               sem_ss, sem_sr, sem_ys, sem_yr, sem_out):
    ep = lax.axis_index('ep')
    ty = lax.axis_index('tp')
    cx = ep // 2
    c = ep % 2
    rF = 1 + c
    rS = 2 - c
    my_rows = pl.ds(pl.multiple_of(c * HALF, HALF), HALF)
    other_rows = pl.ds(pl.multiple_of((1 - c) * HALF, HALF), HALF)

    def dev(r, flip):
        nx = 1 - cx if r & 1 else cx
        nc = 1 - c if flip else c
        ny = 1 - ty if r & 2 else ty
        return {'ep': nx * 2 + nc, 'tp': ny}

    partner = dev(0, True)
    dev_f = {'ep': (cx * c + (1 - cx) * (1 - c)) * 2 + c, 'tp': ty * (1 - c) + (1 - ty) * c}
    dev_s = {'ep': (cx * (1 - c) + (1 - cx) * c) * 2 + c, 'tp': ty * c + (1 - ty) * (1 - c)}

    def rcopy(src, dst, ssem, rsem, device):
        return pltpu.make_async_remote_copy(src_ref=src, dst_ref=dst, send_sem=ssem, recv_sem=rsem,
                                            device_id=device, device_id_type=MESH)

    def w_copies(g):
        e = g % EL
        s = g % WSLOTS
        return (pltpu.make_async_copy(wg_hbm.at[e], wgv.at[s], sem_w.at[s, 0]),
                pltpu.make_async_copy(wu_hbm.at[e], wuv.at[s], sem_w.at[s, 1]))

    def wd_copy(u):
        col = pl.ds(pl.multiple_of((u % NCH) * CH, CH), CH)
        return pltpu.make_async_copy(wd_hbm.at[:, :, col], wdv.at[u % 2], sem_wd.at[u % 2])

    def c_f(p):
        return rcopy(xa.at[p, 0, my_rows], xa.at[p, rF, my_rows], sem_as.at[p, 0], sem_ar.at[p, 0], dev_f)

    def c_s(p):
        return rcopy(xa.at[p, 0, my_rows], xa.at[p, rS, my_rows], sem_as.at[p, 1], sem_ar.at[p, 1], dev_s)

    def c_d(p):
        return rcopy(xa.at[p, rF, my_rows], xa.at[p, 3, my_rows], sem_as.at[p, 2], sem_ar.at[p, 2], dev_s)

    def c_pair(p, r):
        return rcopy(xa.at[p, r, my_rows], xa.at[p, r, my_rows], sem_ds.at[p, r], sem_dr.at[p, r], partner)

    own_first = rcopy(xa.at[c, 0, other_rows], xa.at[c, 0, other_rows], sem_os.at[0], sem_or.at[0], partner)
    own_second = rcopy(xa.at[c, 0, my_rows], xa.at[c, 0, my_rows], sem_os.at[1], sem_or.at[1], partner)

    x_load = pltpu.make_async_copy(x_hbm, xa.at[c, 0], sem_x)
    x_load.start()
    for g in range(WSLOTS):
        for cp in w_copies(g):
            cp.start()
    for u in range(2):
        wd_copy(u).start()

    barrier = pltpu.get_barrier_semaphore()
    peers = [(r, flip) for r in range(4) for flip in (False, True) if (r, flip) != (0, False)]
    for r, flip in peers:
        pl.semaphore_signal(barrier, inc=1, device_id=dev(r, flip), device_id_type=MESH)
    pl.semaphore_wait(barrier, len(peers))

    rt_sends = [rcopy(rt_ref, rtb.at[c * 4 + r], sem_rs.at[r, int(flip)], sem_rr.at[c * 4 + r], dev(r, flip))
                for r, flip in peers]
    for cp in rt_sends:
        cp.start()
    x_load.wait()
    own_first.start()
    own_second.start()

    @pl.when(c == 1)
    def _():
        own_first.wait_recv()

    c_f(0).start()
    c_s(0).start()

    rtb[c * 4] = rt_ref[...]
    t_row = lax.broadcasted_iota(jnp.int32, (ROWS, ROWS), 0)
    t_col = lax.broadcasted_iota(jnp.int32, (ROWS, ROWS), 1)
    utri[...] = jnp.where(t_row < t_col, 1.0, 0.0).astype(jnp.bfloat16)
    for r, flip in peers:
        b = (1 - c if flip else c) * 4 + r
        pltpu.make_async_copy(rt_ref, rtb.at[b], sem_rr.at[b]).wait()
    for cp in rt_sends:
        cp.wait_send()

    q_iota = lax.broadcasted_iota(jnp.int32, (CAP, ROWS), 0).astype(jnp.float32)

    def build(b, _):
        p = b // 4
        r = b % 4
        e_iota = (lax.broadcasted_iota(jnp.int32, (EL, ROWS), 0) + ep * EL).astype(jnp.float32)
        chosen = jnp.zeros((EL, ROWS), jnp.float32)
        gate = jnp.zeros((EL, ROWS), jnp.float32)
        for j in range(8):
            hit = rtb[b, j:j + 1, :] == e_iota
            chosen = jnp.where(hit, 1.0, chosen)
            gate = jnp.where(hit, rtb[b, 8 + j:9 + j, :], gate)
        rank = jnp.dot(chosen.astype(jnp.bfloat16), utri[...], preferred_element_type=jnp.float32)
        kk = jnp.where(chosen > 0.0, rank, -1.0)
        key[b] = kk
        hots = []
        for e in range(EL):
            hit = kk[e:e + 1, :] == q_iota
            hots.append(jnp.where(hit, 1.0, 0.0))
            gsum = jnp.sum(jnp.where(hit, gate[e:e + 1, :], 0.0), axis=1, keepdims=True)
            gp[p, e, pl.ds(pl.multiple_of(r * CAP, CAP), CAP), :] = jnp.broadcast_to(gsum, (CAP, 128))
        dt[b] = jnp.concatenate(hots, axis=0).T.astype(jnp.bfloat16)
        return 0

    lax.fori_loop(0, 8, build, 0)

    c_f(0).wait()
    c_d(0).start()
    c_pair(0, rF).start()

    @pl.when(c == 0)
    def _():
        own_first.wait_recv()

    c_f(1).start()
    c_s(1).start()
    c_s(0).wait()
    c_pair(0, rS).start()
    own_first.wait_send()
    own_second.wait()
    c_d(0).wait()
    c_pair(0, 3).start()
    for r in (1, 2, 3):
        c_pair(0, r).wait()

    def pair_step(p, i):
        for r in range(4):
            hots = [jnp.where(key[p * 4 + r, pl.ds(2 * i + j, 1), :] == q_iota, 1.0, 0.0) for j in range(2)]
            hot = jnp.concatenate(hots, axis=0).astype(jnp.bfloat16)
            for n in range(4):
                cols = slice(n * 512, (n + 1) * 512)
                res = jnp.dot(hot, xa[p, r, :, cols], preferred_element_type=jnp.float32).astype(jnp.bfloat16)
                for j in range(2):
                    xdp[j, r * CAP:(r + 1) * CAP, cols] = res[j * CAP:(j + 1) * CAP]
        for j in range(2):
            e = 2 * i + j
            g = p * EL + e
            for cp in w_copies(g):
                cp.wait()
            s = g % WSLOTS
            for n in range(2):
                cols = slice(n * 256, (n + 1) * 256)
                a = jnp.dot(xdp[j], wgv[s, :, cols], preferred_element_type=jnp.float32)
                b = jnp.dot(xdp[j], wuv[s, :, cols], preferred_element_type=jnp.float32)
                hb[p, e, :, cols] = (a * jax.nn.sigmoid(a) * b).astype(jnp.bfloat16)

            @pl.when(g + WSLOTS < 2 * EL)
            def _():
                for cp in w_copies(g + WSLOTS):
                    cp.start()

    def phase0(i, _):
        pair_step(0, i)

        @pl.when(i == 3)
        def _():
            c_f(1).wait()
            c_d(1).start()
            c_pair(1, rF).start()

        @pl.when(i == 5)
        def _():
            c_s(1).wait()
            c_pair(1, rS).start()
        return 0

    lax.fori_loop(0, EL // 2, phase0, 0)

    def k_pair(u):
        s = u % 2
        return rcopy(ps.at[s], dr.at[s], sem_ps.at[s], sem_pr.at[s], partner)

    def k_first(u, which):
        s = u % 3
        src = pm.at[s, 3] if which == 0 else pm.at[s, rF]
        return rcopy(src, rf.at[s, which], sem_fs.at[s, which], sem_fr.at[s, which], dev_f)

    def k_second(u):
        return rcopy(pm.at[u % 3, rS], rs.at[u % 2], sem_ss.at[u % 2], sem_sr.at[u % 2], dev_s)

    def k_out(k):
        cols = pl.ds(pl.multiple_of(k * CH, CH), CH)
        return rcopy(yst.at[:, cols], yv.at[my_rows, cols], sem_ys.at[k], sem_yr.at[k], partner)

    def stage1(u):
        k_pair(u).wait()
        s = u % 3
        for r in (3, 1, 2, 0):
            pm[s, r] = pm[s, r] + dr[u % 2, r]
        k_first(u, 0).start()
        k_first(u, 1).start()

    def stage2(u):
        k_first(u, 0).wait()
        s = u % 3
        pm[s, rS] = pm[s, rS] + rf[s, 0]
        k_second(u).start()

    def stage3(u):
        k_first(u, 1).wait()
        k_second(u).wait()
        s = u % 3
        k = u % NCH
        cols = pl.ds(pl.multiple_of(k * CH, CH), CH)
        tot = (pm[s, 0] + rf[s, 1] + rs[u % 2]).astype(jnp.bfloat16)

        @pl.when(c == u // NCH)
        def _():
            yv[my_rows, cols] = tot

        @pl.when(c != u // NCH)
        def _():
            yst[:, cols] = tot
            k_out(k).start()

    def compute(u):
        p = u // NCH
        s2 = u % 2
        s3 = u % 3
        wd_copy(u).wait()

        def down(e2, _):
            for j in range(2):
                e = 2 * e2 + j
                o = jnp.dot(hb[p, e], wdv[s2, e], preferred_element_type=jnp.float32)
                g = gp[p, e]
                o = o * jnp.concatenate([g, g], axis=1)
                hi = o.astype(jnp.bfloat16)
                rest = o - hi.astype(jnp.float32)
                mid = rest.astype(jnp.bfloat16)
                lo = (rest - mid.astype(jnp.float32)).astype(jnp.bfloat16)
                rows = pl.ds(pl.multiple_of(e * CAP, CAP), CAP)
                for r in range(4):
                    part = slice(r * CAP, (r + 1) * CAP)
                    ob[0, r, rows, :] = hi[part]
                    ob[1, r, rows, :] = mid[part]
                    ob[2, r, rows, :] = lo[part]
            return 0

        lax.fori_loop(0, EL // 2, down, 0)

        @pl.when(u + 2 < UNITS)
        def _():
            wd_copy(u + 2).start()

        def combine(rows, dst, s):
            def body(r, _):
                sel = dt[p * 4 + r, rows, :]
                acc = jnp.dot(sel, ob[0, r], preferred_element_type=jnp.float32)
                acc += jnp.dot(sel, ob[1, r], preferred_element_type=jnp.float32)
                acc += jnp.dot(sel, ob[2, r], preferred_element_type=jnp.float32)
                dst[s, r] = acc
                return 0
            lax.fori_loop(0, 4, body, 0)

        combine(other_rows, ps, s2)
        k_pair(u).start()
        combine(my_rows, pm, s3)

    def unit(i, _):
        @pl.when(i >= 3)
        def _():
            stage3(i - 3)

        @pl.when((i >= 2) & (i < UNITS + 2))
        def _():
            stage2(i - 2)

        @pl.when((i >= 1) & (i < UNITS + 1))
        def _():
            stage1(i - 1)

        @pl.when(i < UNITS)
        def _():
            compute(i)

        @pl.when(i == 0)
        def _():
            c_d(1).wait()
            c_pair(1, 3).start()
            for r in (1, 2, 3):
                c_pair(1, r).wait()

        @pl.when(i < EL // 2)
        def _():
            pair_step(1, i)
        return 0

    lax.fori_loop(0, UNITS + 3, unit, 0)

    for k in range(NCH):
        k_out(k).wait()
    out = pltpu.make_async_copy(yv, y_hbm, sem_out)
    out.start()
    out.wait()


def solution(mesh):
    row_spec = P(('dp', 'ep', 'tp'), None)
    bf, f32 = jnp.bfloat16, jnp.float32

    def local_moe(x, ids, gate, wg, wu, wd):
        rt = jnp.concatenate([ids.T.astype(f32), gate.T], axis=0)
        anyspec = pl.BlockSpec(memory_space=pl.ANY)
        dma = pltpu.SemaphoreType.DMA
        return pl.pallas_call(
            moe_kernel,
            out_shape=jax.ShapeDtypeStruct((ROWS, DM), bf),
            in_specs=[pl.BlockSpec(memory_space=pltpu.VMEM)] + [anyspec] * 4,
            out_specs=anyspec,
            scratch_shapes=[
                pltpu.VMEM((2, 4, ROWS, DM), bf),
                pltpu.VMEM((8, 16, ROWS), f32),
                pltpu.VMEM((8, EL, ROWS), f32),
                pltpu.VMEM((8, ROWS, EL * CAP), bf),
                pltpu.VMEM((2, EL, 4 * CAP, 128), f32),
                pltpu.VMEM((ROWS, ROWS), bf),
                pltpu.VMEM((2, 4 * CAP, DM), bf),
                pltpu.VMEM((2, EL, 4 * CAP, FF), bf),
                pltpu.VMEM((WSLOTS, DM, FF), bf),
                pltpu.VMEM((WSLOTS, DM, FF), bf),
                pltpu.VMEM((2, EL, FF, CH), bf),
                pltpu.VMEM((3, 4, EL * CAP, CH), bf),
                pltpu.VMEM((3, 4, HALF, CH), f32),
                pltpu.VMEM((2, 4, HALF, CH), f32),
                pltpu.VMEM((2, 4, HALF, CH), f32),
                pltpu.VMEM((3, 2, HALF, CH), f32),
                pltpu.VMEM((2, HALF, CH), f32),
                pltpu.VMEM((ROWS, DM), bf),
                pltpu.VMEM((HALF, DM), bf),
                dma, dma((WSLOTS, 2)), dma((2,)), dma((4, 2)), dma((8,)), dma((2,)), dma((2,)),
                dma((2, 3)), dma((2, 3)), dma((2, 4)), dma((2, 4)), dma((2,)), dma((2,)),
                dma((3, 2)), dma((3, 2)), dma((2,)), dma((2,)), dma((NCH,)), dma((NCH,)), dma,
            ],
            compiler_params=pltpu.CompilerParams(
                collective_id=0, has_side_effects=True, vmem_limit_bytes=67_043_328),
        )(rt, x, wg, wu, wd)

    return jax.shard_map(
        local_moe, mesh=mesh,
        in_specs=(row_spec, row_spec, row_spec, P('ep', None, 'tp'), P('ep', None, 'tp'), P('ep', 'tp', None)),
        out_specs=row_spec, check_vma=False)
```

time: 502 us -> 226 us (0.45)
  Pallas kernels: 0 us -> 221 us
  waiting for transfers between devices: 147 us -> 0 us
  other arithmetic: 136 us -> 2.02 us
  matrix products: 89 us -> 0 us
  local copies, waits for them, and re-layouts: 89.3 us -> 2.73 us
  blocking collectives: 26.1 us -> 0 us
  between operations: 13.5 us -> 0.01 us
    pallas_call x0 -> x1, Pallas kernels: none -> 221 us  [local_moe(): pl.pallas_call(moe_kernel, out_shape=jax.ShapeDtypeStruct((ROWS, DM), bf)...]
    reduce_scatter x1 -> x0, waiting for transfers between devices: 147 us -> none  [local_moe(): lax.psum_scatter(partial_sum, ('ep', 'tp'), scatter_dimension=0, tiled=True)]
    dot_general x2 -> x0, matrix products: 89 us -> none  [the longest x1 53.3 us: local_moe(): jnp.einsum('ecf,efd->ecd', hidden, w_down, preferred_element_type=jnp.flo...]
    gather x2 -> x0, local copies, waits for them, and re-layouts: 86.8 us -> none  [the longest x1 52.5 us: local_moe(): x_rows = x_all[tok_rows].reshape(e_local, expert_cap, -1)]
    scatter-add x1 -> x0, other arithmetic: 86.8 us -> none  [local_moe(): partial_sum = jax.ops.segment_sum(out_rows, tok_rows, num_segments=num_tok)]
    mul x1 -> x0, other arithmetic: 34.5 us -> none  [local_moe(): out_rows = out_rows.reshape(local_pairs, -1) * gate_rows[:, None]]
    all_gather x2 -> x0, blocking collectives: 26.1 us -> none  [the longest x1 14.2 us: local_moe(): gate_all = lax.all_gather(gate_local, ('ep', 'tp'), tiled=True)]
    sort x1 -> x0, other arithmetic: 11.3 us -> none  [local_moe(): jnp.argsort(jnp.where(is_local, local_ids, e_local), stable=True)]
  transfers between devices with their start and end apart: 2 -> 0, of which waited for: 1 -> 0; matrix products, arithmetic and copies ran while one was open for 10% -> 0% of each run, Pallas kernels for 0% -> 0%
where the time goes in v1:
time: 226 us
  Pallas kernels  221 us (98%)
  local copies, waits for them, and re-layouts  2.73 us (1%)
    pallas_call x1, Pallas kernels, local_moe(): pl.pallas_call(moe_kernel, out_shape=jax.ShapeDtypeStruct((ROWS, DM), bf)...  221 us

profile of v1, /device:TPU:0, one launch (start us, length us, event | category | flops | bytes accessed | tf_op | source)
XLA Modules:
  0.0 225.6 jit_solution(17930302962013347777)
XLA Ops:
  0.0 0.7 convert_bitcast_fusion
  0.7 1.3 pad_maximum_fusion.rt_ref
  2.0 220.8 %shard_map.64 = bf16[384,2048]{1,0:T(8,128)(2,1)} custom-call(f32[16,384]{1,0:T(8,128)} %pad_maximum_fusion.rt_ref, bf16[384,2048]{1,0:T(8,128)(2,1)} %x_hbm.1, bf16[16,2048,512]{2,1,0:T(8,128)(2,1)} %wg_hbm.1, bf16[16,2048,512]{2,1,0:T(8,128)(2,1)} %wu_hbm.1, bf16[16,512,2048]{2,1,0:T(8,128)(2,1)} %wd_hbm.1), custom_call_target="tpu_custom_call" | custom-call | tf_op jit(solution)/shard_map/pallas_call | solution.py:341
  222.8 2.7 %copy.8 = bf16[384,2048]{1,0:T(8,128)(2,1)} copy(bf16[384,2048]{1,0:T(8,128)(2,1)} %shard_map.64) | data formatting | bytes 3145728

commit v2 on v1

--- a/solution.py
+++ b/solution.py
@@ -147,18 +147,18 @@
     def _():
         own_first.wait_recv()
 
-    c_f(1).start()
-    c_s(1).start()
     c_s(0).wait()
     c_pair(0, rS).start()
     own_first.wait_send()
     own_second.wait()
     c_d(0).wait()
     c_pair(0, 3).start()
+    c_f(1).start()
+    c_s(1).start()
     for r in (1, 2, 3):
         c_pair(0, r).wait()
 
-    def pair_step(p, i):
+    def dispatch(p, i):
         for r in range(4):
             hots = [jnp.where(key[p * 4 + r, pl.ds(2 * i + j, 1), :] == q_iota, 1.0, 0.0) for j in range(2)]
             hot = jnp.concatenate(hots, axis=0).astype(jnp.bfloat16)
@@ -167,6 +167,8 @@
                 res = jnp.dot(hot, xa[p, r, :, cols], preferred_element_type=jnp.float32).astype(jnp.bfloat16)
                 for j in range(2):
                     xdp[j, r * CAP:(r + 1) * CAP, cols] = res[j * CAP:(j + 1) * CAP]
+
+    def experts(p, i):
         for j in range(2):
             e = 2 * i + j
             g = p * EL + e
@@ -185,15 +187,16 @@
                     cp.start()
 
     def phase0(i, _):
-        pair_step(0, i)
-
-        @pl.when(i == 3)
+        dispatch(0, i)
+        experts(0, i)
+
+        @pl.when(i == 5)
         def _():
             c_f(1).wait()
             c_d(1).start()
             c_pair(1, rF).start()
 
-        @pl.when(i == 5)
+        @pl.when(i == 6)
         def _():
             c_s(1).wait()
             c_pair(1, rS).start()
@@ -203,12 +206,13 @@
 
     def k_pair(u):
         s = u % 2
-        return rcopy(ps.at[s], dr.at[s], sem_ps.at[s], sem_pr.at[s], partner)
+        return rcopy(ps, dr.at[s], sem_ps, sem_pr.at[s], partner)
 
     def k_first(u, which):
         s = u % 3
+        t = u % 4
         src = pm.at[s, 3] if which == 0 else pm.at[s, rF]
-        return rcopy(src, rf.at[s, which], sem_fs.at[s, which], sem_fr.at[s, which], dev_f)
+        return rcopy(src, rf.at[t, which], sem_fs.at[t, which], sem_fr.at[t, which], dev_f)
 
     def k_second(u):
         return rcopy(pm.at[u % 3, rS], rs.at[u % 2], sem_ss.at[u % 2], sem_sr.at[u % 2], dev_s)
@@ -228,16 +232,17 @@
     def stage2(u):
         k_first(u, 0).wait()
         s = u % 3
-        pm[s, rS] = pm[s, rS] + rf[s, 0]
+        pm[s, rS] = pm[s, rS] + rf[u % 4, 0]
         k_second(u).start()
+        k_first(u, 1).wait()
+        pm[s, 0] = pm[s, 0] + rf[u % 4, 1]
 
     def stage3(u):
-        k_first(u, 1).wait()
         k_second(u).wait()
         s = u % 3
         k = u % NCH
         cols = pl.ds(pl.multiple_of(k * CH, CH), CH)
-        tot = (pm[s, 0] + rf[s, 1] + rs[u % 2]).astype(jnp.bfloat16)
+        tot = (pm[s, 0] + rs[u % 2]).astype(jnp.bfloat16)
 
         @pl.when(c == u // NCH)
         def _():
@@ -254,43 +259,42 @@
         s3 = u % 3
         wd_copy(u).wait()
 
-        def down(e2, _):
-            for j in range(2):
-                e = 2 * e2 + j
-                o = jnp.dot(hb[p, e], wdv[s2, e], preferred_element_type=jnp.float32)
-                g = gp[p, e]
-                o = o * jnp.concatenate([g, g], axis=1)
-                hi = o.astype(jnp.bfloat16)
-                rest = o - hi.astype(jnp.float32)
-                mid = rest.astype(jnp.bfloat16)
-                lo = (rest - mid.astype(jnp.float32)).astype(jnp.bfloat16)
-                rows = pl.ds(pl.multiple_of(e * CAP, CAP), CAP)
-                for r in range(4):
-                    part = slice(r * CAP, (r + 1) * CAP)
-                    ob[0, r, rows, :] = hi[part]
-                    ob[1, r, rows, :] = mid[part]
-                    ob[2, r, rows, :] = lo[part]
-            return 0
-
-        lax.fori_loop(0, EL // 2, down, 0)
+        for e in range(EL):
+            o = jnp.dot(hb[p, e], wdv[s2, e], preferred_element_type=jnp.float32)
+            g = gp[p, e]
+            o = o * jnp.concatenate([g, g], axis=1)
+            hi = o.astype(jnp.bfloat16)
+            rest = o - hi.astype(jnp.float32)
+            mid = rest.astype(jnp.bfloat16)
+            lo = (rest - mid.astype(jnp.float32)).astype(jnp.bfloat16)
+            rows = slice(e * CAP, (e + 1) * CAP)
+            for r in range(4):
+                part = slice(r * CAP, (r + 1) * CAP)
+                ob[0, r, rows, :] = hi[part]
+                ob[1, r, rows, :] = mid[part]
+                ob[2, r, rows, :] = lo[part]
 
         @pl.when(u + 2 < UNITS)
         def _():
             wd_copy(u + 2).start()
 
-        def combine(rows, dst, s):
-            def body(r, _):
+        def combine(rows, store):
+            for r in range(4):
                 sel = dt[p * 4 + r, rows, :]
                 acc = jnp.dot(sel, ob[0, r], preferred_element_type=jnp.float32)
                 acc += jnp.dot(sel, ob[1, r], preferred_element_type=jnp.float32)
                 acc += jnp.dot(sel, ob[2, r], preferred_element_type=jnp.float32)
-                dst[s, r] = acc
-                return 0
-            lax.fori_loop(0, 4, body, 0)
-
-        combine(other_rows, ps, s2)
+                store(r, acc)
+
+        def store_other(r, acc):
+            ps[r] = acc
+
+        def store_mine(r, acc):
+            pm[s3, r] = acc
+
+        combine(other_rows, store_other)
         k_pair(u).start()
-        combine(my_rows, pm, s3)
+        combine(my_rows, store_mine)
 
     def unit(i, _):
         @pl.when(i >= 3)
@@ -300,10 +304,6 @@
         @pl.when((i >= 2) & (i < UNITS + 2))
         def _():
             stage2(i - 2)
-
-        @pl.when((i >= 1) & (i < UNITS + 1))
-        def _():
-            stage1(i - 1)
 
         @pl.when(i < UNITS)
         def _():
@@ -318,7 +318,15 @@
 
         @pl.when(i < EL // 2)
         def _():
-            pair_step(1, i)
+            dispatch(1, i)
+
+        @pl.when(i < UNITS)
+        def _():
+            stage1(i)
+
+        @pl.when(i < EL // 2)
+        def _():
+            experts(1, i)
         return 0
 
     lax.fori_loop(0, UNITS + 3, unit, 0)
@@ -357,15 +365,15 @@
                 pltpu.VMEM((2, EL, FF, CH), bf),
                 pltpu.VMEM((3, 4, EL * CAP, CH), bf),
                 pltpu.VMEM((3, 4, HALF, CH), f32),
+                pltpu.VMEM((4, HALF, CH), f32),
                 pltpu.VMEM((2, 4, HALF, CH), f32),
-                pltpu.VMEM((2, 4, HALF, CH), f32),
-                pltpu.VMEM((3, 2, HALF, CH), f32),
+                pltpu.VMEM((4, 2, HALF, CH), f32),
                 pltpu.VMEM((2, HALF, CH), f32),
                 pltpu.VMEM((ROWS, DM), bf),
                 pltpu.VMEM((HALF, DM), bf),
                 dma, dma((WSLOTS, 2)), dma((2,)), dma((4, 2)), dma((8,)), dma((2,)), dma((2,)),
-                dma((2, 3)), dma((2, 3)), dma((2, 4)), dma((2, 4)), dma((2,)), dma((2,)),
-                dma((3, 2)), dma((3, 2)), dma((2,)), dma((2,)), dma((NCH,)), dma((NCH,)), dma,
+                dma((2, 3)), dma((2, 3)), dma((2, 4)), dma((2, 4)), dma, dma((2,)),
+                dma((4, 2)), dma((4, 2)), dma((2,)), dma((2,)), dma((NCH,)), dma((NCH,)), dma,
             ],
             compiler_params=pltpu.CompilerParams(
                 collective_id=0, has_side_effects=True, vmem_limit_bytes=67_043_328),

time: 226 us -> 195 us (0.86)
  Pallas kernels: 221 us -> 190 us
    pallas_call x1, Pallas kernels: 221 us -> 190 us  [local_moe(): pl.pallas_call(moe_kernel, out_shape=jax.ShapeDtypeStruct((ROWS, DM), bf)...]
where the time goes in v2:
time: 195 us; the launch traced here: 194 us
  Pallas kernels  190 us (97%)
  local copies, waits for them, and re-layouts  2.73 us (1%)
  other arithmetic  2.02 us (1%)
    pallas_call x1, Pallas kernels, local_moe(): pl.pallas_call(moe_kernel, out_shape=jax.ShapeDtypeStruct((ROWS, DM), bf)...  190 us

profile of v2, /device:TPU:0, one launch (start us, length us, event | category | flops | bytes accessed | tf_op | source)
XLA Modules:
  0.0 194.4 jit_solution(2953275757909525964)
XLA Ops:
  0.0 0.7 convert_bitcast_fusion
  0.7 1.3 pad_maximum_fusion.rt_ref
  2.0 189.7 %shard_map.64 = bf16[384,2048]{1,0:T(8,128)(2,1)} custom-call(f32[16,384]{1,0:T(8,128)} %pad_maximum_fusion.rt_ref, bf16[384,2048]{1,0:T(8,128)(2,1)} %x_hbm.1, bf16[16,2048,512]{2,1,0:T(8,128)(2,1)} %wg_hbm.1, bf16[16,2048,512]{2,1,0:T(8,128)(2,1)} %wu_hbm.1, bf16[16,512,2048]{2,1,0:T(8,128)(2,1)} %wd_hbm.1), custom_call_target="tpu_custom_call" | custom-call | tf_op jit(solution)/shard_map/pallas_call | solution.py:349
  191.7 2.7 %copy.8 = bf16[384,2048]{1,0:T(8,128)(2,1)} copy(bf16[384,2048]{1,0:T(8,128)(2,1)} %shard_map.64) | data formatting | bytes 3145728

commit v3 on v2

--- a/solution.py
+++ b/solution.py
@@ -10,6 +10,7 @@
 MESH = pl.DeviceIdType.MESH
 ROWS = 384
 HALF = 192
+PIECE = 96
 CAP = 48
 DM = 2048
 FF = 512
@@ -22,10 +23,10 @@
 
 def moe_kernel(rt_ref, x_hbm, wg_hbm, wu_hbm, wd_hbm, y_hbm,
                xa, rtb, key, dt, gp, utri, xdp, hb, wgv, wuv, wdv, ob,
-               pm, ps, dr, rf, rs, yv, yst,
+               pm, ps, dr, rf, rs, yst,
                sem_x, sem_w, sem_wd, sem_rs, sem_rr, sem_os, sem_or,
                sem_as, sem_ar, sem_ds, sem_dr, sem_ps, sem_pr, sem_fs, sem_fr,
-               sem_ss, sem_sr, sem_ys, sem_yr, sem_out):
+               sem_ss, sem_sr, sem_ys, sem_yr, sem_yl):
     ep = lax.axis_index('ep')
     ty = lax.axis_index('tp')
     cx = ep // 2
@@ -59,17 +60,37 @@
         col = pl.ds(pl.multiple_of((u % NCH) * CH, CH), CH)
         return pltpu.make_async_copy(wd_hbm.at[:, :, col], wdv.at[u % 2], sem_wd.at[u % 2])
 
-    def c_f(p):
-        return rcopy(xa.at[p, 0, my_rows], xa.at[p, rF, my_rows], sem_as.at[p, 0], sem_ar.at[p, 0], dev_f)
-
-    def c_s(p):
-        return rcopy(xa.at[p, 0, my_rows], xa.at[p, rS, my_rows], sem_as.at[p, 1], sem_ar.at[p, 1], dev_s)
-
-    def c_d(p):
-        return rcopy(xa.at[p, rF, my_rows], xa.at[p, 3, my_rows], sem_as.at[p, 2], sem_ar.at[p, 2], dev_s)
-
-    def c_pair(p, r):
-        return rcopy(xa.at[p, r, my_rows], xa.at[p, r, my_rows], sem_ds.at[p, r], sem_dr.at[p, r], partner)
+    def piece(q):
+        return pl.ds(pl.multiple_of(c * HALF + q * PIECE, PIECE), PIECE)
+
+    def c_f(p, q):
+        return rcopy(xa.at[p, 0, piece(q)], xa.at[p, rF, piece(q)], sem_as.at[p, 0, q], sem_ar.at[p, 0, q], dev_f)
+
+    def c_s(p, q):
+        return rcopy(xa.at[p, 0, piece(q)], xa.at[p, rS, piece(q)], sem_as.at[p, 1, q], sem_ar.at[p, 1, q], dev_s)
+
+    def c_d(p, q):
+        return rcopy(xa.at[p, rF, piece(q)], xa.at[p, 3, piece(q)], sem_as.at[p, 2, q], sem_ar.at[p, 2, q], dev_s)
+
+    def c_pair(p, r, q):
+        return rcopy(xa.at[p, r, piece(q)], xa.at[p, r, piece(q)], sem_ds.at[p, r, q], sem_dr.at[p, r, q], partner)
+
+    def rows_first(p, q):
+        c_f(p, q).wait()
+        c_d(p, q).start()
+        c_pair(p, rF, q).start()
+
+    def rows_second(p, q):
+        c_s(p, q).wait()
+        c_pair(p, rS, q).start()
+
+    def rows_third(p, q):
+        c_d(p, q).wait()
+        c_pair(p, 3, q).start()
+
+    def rows_done(p, r):
+        for q in range(2):
+            c_pair(p, r, q).wait()
 
     own_first = rcopy(xa.at[c, 0, other_rows], xa.at[c, 0, other_rows], sem_os.at[0], sem_or.at[0], partner)
     own_second = rcopy(xa.at[c, 0, my_rows], xa.at[c, 0, my_rows], sem_os.at[1], sem_or.at[1], partner)
@@ -79,8 +100,6 @@
     for g in range(WSLOTS):
         for cp in w_copies(g):
             cp.start()
-    for u in range(2):
-        wd_copy(u).start()
 
     barrier = pltpu.get_barrier_semaphore()
     peers = [(r, flip) for r in range(4) for flip in (False, True) if (r, flip) != (0, False)]
@@ -88,10 +107,16 @@
         pl.semaphore_signal(barrier, inc=1, device_id=dev(r, flip), device_id_type=MESH)
     pl.semaphore_wait(barrier, len(peers))
 
-    rt_sends = [rcopy(rt_ref, rtb.at[c * 4 + r], sem_rs.at[r, int(flip)], sem_rr.at[c * 4 + r], dev(r, flip))
-                for r, flip in peers]
-    for cp in rt_sends:
-        cp.start()
+    def rt_link(r):
+        return rcopy(rt_ref, rtb.at[c * 4 + r], sem_rs.at[r, 0], sem_rr.at[c * 4 + r], dev(r, False))
+
+    def rt_pair(r):
+        b = c * 4 + r
+        return rcopy(rt_ref if r == 0 else rtb.at[b], rtb.at[b], sem_rs.at[r, 1], sem_rr.at[b], partner)
+
+    for r in (3, 1, 2):
+        rt_link(r).start()
+    rt_pair(0).start()
     x_load.wait()
     own_first.start()
     own_second.start()
@@ -100,18 +125,21 @@
     def _():
         own_first.wait_recv()
 
-    c_f(0).start()
-    c_s(0).start()
+    for q in range(2):
+        c_f(0, q).start()
+        c_s(0, q).start()
 
     rtb[c * 4] = rt_ref[...]
     t_row = lax.broadcasted_iota(jnp.int32, (ROWS, ROWS), 0)
     t_col = lax.broadcasted_iota(jnp.int32, (ROWS, ROWS), 1)
     utri[...] = jnp.where(t_row < t_col, 1.0, 0.0).astype(jnp.bfloat16)
-    for r, flip in peers:
-        b = (1 - c if flip else c) * 4 + r
+    for r in (1, 2, 3):
+        rt_link(r).wait()
+        rt_pair(r).start()
+    for r in range(4):
+        rt_pair(r).wait_send()
+        b = (1 - c) * 4 + r
         pltpu.make_async_copy(rt_ref, rtb.at[b], sem_rr.at[b]).wait()
-    for cp in rt_sends:
-        cp.wait_send()
 
     q_iota = lax.broadcasted_iota(jnp.int32, (CAP, ROWS), 0).astype(jnp.float32)
 
@@ -139,27 +167,77 @@
 
     lax.fori_loop(0, 8, build, 0)
 
-    c_f(0).wait()
-    c_d(0).start()
-    c_pair(0, rF).start()
+    own_first.wait_send()
+    own_second.wait()
 
     @pl.when(c == 0)
     def _():
         own_first.wait_recv()
 
-    c_s(0).wait()
-    c_pair(0, rS).start()
-    own_first.wait_send()
-    own_second.wait()
-    c_d(0).wait()
-    c_pair(0, 3).start()
-    c_f(1).start()
-    c_s(1).start()
-    for r in (1, 2, 3):
-        c_pair(0, r).wait()
-
-    def dispatch(p, i):
-        for r in range(4):
+    def put(e, q, r, val):
+        rows = pl.ds(pl.multiple_of(r * CAP, CAP), CAP)
+        if e < 8:
+            rows = pl.ds(pl.multiple_of((q % 2) * HALF + r * CAP, CAP), CAP)
+            wdv[e // 4, (e % 4) * 4 + q // 2, rows, :] = val
+        elif e < 14:
+            rows = pl.ds(pl.multiple_of((q % 4) * HALF + r * CAP, CAP), CAP)
+            ob[(e - 8) * 2 + q // 4, rows, :] = val
+        else:
+            xdp[e - 14, rows, q * 256:(q + 1) * 256] = val
+
+    def dispatch_block(r, _):
+        @pl.when(r == 1)
+        def _():
+            rows_first(0, 0)
+            rows_second(0, 0)
+            rows_first(0, 1)
+            c_s(1, 0).start()
+            c_s(1, 1).start()
+            rows_second(0, 1)
+            rows_done(0, 1)
+            rows_done(0, 2)
+
+        @pl.when(r == 3)
+        def _():
+            rows_third(0, 0)
+            rows_third(0, 1)
+            c_f(1, 0).start()
+            c_f(1, 1).start()
+            rows_done(0, 3)
+
+        kk = key[r]
+        for eg in range(4):
+            hots = [jnp.where(kk[e:e + 1, :] == q_iota, 1.0, 0.0) for e in range(eg * 4, eg * 4 + 4)]
+            hot = jnp.concatenate(hots, axis=0).astype(jnp.bfloat16)
+            for n in range(4):
+                res = jnp.dot(hot, xa[0, r, :, n * 512:(n + 1) * 512],
+                              preferred_element_type=jnp.float32).astype(jnp.bfloat16)
+                for j in range(4):
+                    for m in range(2):
+                        put(eg * 4 + j, n * 2 + m, r, res[j * CAP:(j + 1) * CAP, m * 256:(m + 1) * 256])
+        return 0
+
+    lax.fori_loop(0, 4, dispatch_block, 0)
+
+    def expert(p, e, rows_of):
+        g = p * EL + e
+        for cp in w_copies(g):
+            cp.wait()
+        s = g % WSLOTS
+        xe = rows_of()
+        for n in range(2):
+            cols = slice(n * 256, (n + 1) * 256)
+            a = jnp.dot(xe, wgv[s, :, cols], preferred_element_type=jnp.float32)
+            b = jnp.dot(xe, wuv[s, :, cols], preferred_element_type=jnp.float32)
+            hb[p, e, :, cols] = (a * jax.nn.sigmoid(a) * b).astype(jnp.bfloat16)
+
+        @pl.when(g + WSLOTS < 2 * EL)
+        def _():
+            for cp in w_copies(g + WSLOTS):
+                cp.start()
+
+    def dispatch(p, i, blocks):
+        for r in blocks:
             hots = [jnp.where(key[p * 4 + r, pl.ds(2 * i + j, 1), :] == q_iota, 1.0, 0.0) for j in range(2)]
             hot = jnp.concatenate(hots, axis=0).astype(jnp.bfloat16)
             for n in range(4):
@@ -168,41 +246,42 @@
                 for j in range(2):
                     xdp[j, r * CAP:(r + 1) * CAP, cols] = res[j * CAP:(j + 1) * CAP]
 
-    def experts(p, i):
-        for j in range(2):
-            e = 2 * i + j
-            g = p * EL + e
-            for cp in w_copies(g):
-                cp.wait()
-            s = g % WSLOTS
-            for n in range(2):
-                cols = slice(n * 256, (n + 1) * 256)
-                a = jnp.dot(xdp[j], wgv[s, :, cols], preferred_element_type=jnp.float32)
-                b = jnp.dot(xdp[j], wuv[s, :, cols], preferred_element_type=jnp.float32)
-                hb[p, e, :, cols] = (a * jax.nn.sigmoid(a) * b).astype(jnp.bfloat16)
-
-            @pl.when(g + WSLOTS < 2 * EL)
-            def _():
-                for cp in w_copies(g + WSLOTS):
-                    cp.start()
-
-    def phase0(i, _):
-        dispatch(0, i)
-        experts(0, i)
-
-        @pl.when(i == 5)
-        def _():
-            c_f(1).wait()
-            c_d(1).start()
-            c_pair(1, rF).start()
-
-        @pl.when(i == 6)
-        def _():
-            c_s(1).wait()
-            c_pair(1, rS).start()
-        return 0
-
-    lax.fori_loop(0, EL // 2, phase0, 0)
+    def experts_a(e, _):
+        def rows_of():
+            return jnp.concatenate([wdv[e // 4, (e % 4) * 4 + q // 2, (q % 2) * HALF:(q % 2 + 1) * HALF, :]
+                                    for q in range(8)], axis=1)
+        expert(0, e, rows_of)
+
+        @pl.when(e == 3)
+        def _():
+            wd_copy(0).start()
+
+        @pl.when(e == 5)
+        def _():
+            rows_first(1, 0)
+            rows_second(1, 0)
+
+        @pl.when(e == 7)
+        def _():
+            wd_copy(1).start()
+        return 0
+
+    def experts_b(e, _):
+        def rows_of():
+            return jnp.concatenate([ob[(e - 8) * 2 + q // 4, (q % 4) * HALF:(q % 4 + 1) * HALF, :]
+                                    for q in range(8)], axis=1)
+        expert(0, e, rows_of)
+        return 0
+
+    def experts_c(e, _):
+        expert(0, e, lambda: xdp[e - 14])
+        return 0
+
+    lax.fori_loop(0, 8, experts_a, 0)
+    lax.fori_loop(8, 14, experts_b, 0)
+    rows_first(1, 1)
+    rows_second(1, 1)
+    lax.fori_loop(14, 16, experts_c, 0)
 
     def k_pair(u):
         s = u % 2
@@ -219,7 +298,11 @@
 
     def k_out(k):
         cols = pl.ds(pl.multiple_of(k * CH, CH), CH)
-        return rcopy(yst.at[:, cols], yv.at[my_rows, cols], sem_ys.at[k], sem_yr.at[k], partner)
+        return rcopy(yst.at[1, :, cols], y_hbm.at[my_rows, cols], sem_ys.at[k], sem_yr.at[k], partner)
+
+    def k_local(k):
+        cols = pl.ds(pl.multiple_of(k * CH, CH), CH)
+        return pltpu.make_async_copy(yst.at[0, :, cols], y_hbm.at[my_rows, cols], sem_yl.at[k])
 
     def stage1(u):
         k_pair(u).wait()
@@ -246,11 +329,12 @@
 
         @pl.when(c == u // NCH)
         def _():
-            yv[my_rows, cols] = tot
+            yst[0, :, cols] = tot
+            k_local(k).start()
 
         @pl.when(c != u // NCH)
         def _():
-            yst[:, cols] = tot
+            yst[1, :, cols] = tot
             k_out(k).start()
 
     def compute(u):
@@ -270,9 +354,9 @@
             rows = slice(e * CAP, (e + 1) * CAP)
             for r in range(4):
                 part = slice(r * CAP, (r + 1) * CAP)
-                ob[0, r, rows, :] = hi[part]
-                ob[1, r, rows, :] = mid[part]
-                ob[2, r, rows, :] = lo[part]
+                ob[r, rows, :] = hi[part]
+                ob[4 + r, rows, :] = mid[part]
+                ob[8 + r, rows, :] = lo[part]
 
         @pl.when(u + 2 < UNITS)
         def _():
@@ -281,9 +365,9 @@
         def combine(rows, store):
             for r in range(4):
                 sel = dt[p * 4 + r, rows, :]
-                acc = jnp.dot(sel, ob[0, r], preferred_element_type=jnp.float32)
-                acc += jnp.dot(sel, ob[1, r], preferred_element_type=jnp.float32)
-                acc += jnp.dot(sel, ob[2, r], preferred_element_type=jnp.float32)
+                acc = jnp.dot(sel, ob[r], preferred_element_type=jnp.float32)
+                acc += jnp.dot(sel, ob[4 + r], preferred_element_type=jnp.float32)
+                acc += jnp.dot(sel, ob[8 + r], preferred_element_type=jnp.float32)
                 store(r, acc)
 
         def store_other(r, acc):
@@ -309,33 +393,34 @@
         def _():
             compute(i)
 
+        @pl.when(i < EL // 2)
+        def _():
+            dispatch(1, i, (0, 1, 2))
+
+        @pl.when(i < UNITS)
+        def _():
+            stage1(i)
+
         @pl.when(i == 0)
         def _():
-            c_d(1).wait()
-            c_pair(1, 3).start()
-            for r in (1, 2, 3):
-                c_pair(1, r).wait()
+            rows_third(1, 0)
+            rows_third(1, 1)
+            rows_done(1, 3)
 
         @pl.when(i < EL // 2)
         def _():
-            dispatch(1, i)
-
-        @pl.when(i < UNITS)
-        def _():
-            stage1(i)
-
-        @pl.when(i < EL // 2)
-        def _():
-            experts(1, i)
-        return 0
-
+            dispatch(1, i, (3,))
+            for j in range(2):
+                expert(1, 2 * i + j, lambda: xdp[j])
+        return 0
+
+    rows_done(1, 1)
+    rows_done(1, 2)
     lax.fori_loop(0, UNITS + 3, unit, 0)
 
     for k in range(NCH):
+        k_local(k).wait()
         k_out(k).wait()
-    out = pltpu.make_async_copy(yv, y_hbm, sem_out)
-    out.start()
-    out.wait()
 
 
 def solution(mesh):
@@ -363,17 +448,16 @@
                 pltpu.VMEM((WSLOTS, DM, FF), bf),
                 pltpu.VMEM((WSLOTS, DM, FF), bf),
                 pltpu.VMEM((2, EL, FF, CH), bf),
-                pltpu.VMEM((3, 4, EL * CAP, CH), bf),
+                pltpu.VMEM((12, EL * CAP, CH), bf),
                 pltpu.VMEM((3, 4, HALF, CH), f32),
                 pltpu.VMEM((4, HALF, CH), f32),
                 pltpu.VMEM((2, 4, HALF, CH), f32),
                 pltpu.VMEM((4, 2, HALF, CH), f32),
                 pltpu.VMEM((2, HALF, CH), f32),
-                pltpu.VMEM((ROWS, DM), bf),
-                pltpu.VMEM((HALF, DM), bf),
+                pltpu.VMEM((2, HALF, DM), bf),
                 dma, dma((WSLOTS, 2)), dma((2,)), dma((4, 2)), dma((8,)), dma((2,)), dma((2,)),
-                dma((2, 3)), dma((2, 3)), dma((2, 4)), dma((2, 4)), dma, dma((2,)),
-                dma((4, 2)), dma((4, 2)), dma((2,)), dma((2,)), dma((NCH,)), dma((NCH,)), dma,
+                dma((2, 3, 2)), dma((2, 3, 2)), dma((2, 4, 2)), dma((2, 4, 2)), dma, dma((2,)),
+                dma((4, 2)), dma((4, 2)), dma((2,)), dma((2,)), dma((NCH,)), dma((NCH,)), dma((NCH,)),
             ],
             compiler_params=pltpu.CompilerParams(
                 collective_id=0, has_side_effects=True, vmem_limit_bytes=67_043_328),

time: 195 us -> 186 us (0.954)
  Pallas kernels: 190 us -> 181 us
    pallas_call x1, Pallas kernels: 190 us -> 181 us  [local_moe(): pl.pallas_call(moe_kernel, out_shape=jax.ShapeDtypeStruct((ROWS, DM), bf)...]
where the time goes in v3:
time: 186 us
  Pallas kernels  181 us (97%)
  local copies, waits for them, and re-layouts  2.73 us (1%)
  other arithmetic  2.02 us (1%)
    pallas_call x1, Pallas kernels, local_moe(): pl.pallas_call(moe_kernel, out_shape=jax.ShapeDtypeStruct((ROWS, DM), bf)...  181 us

profile of v3, /device:TPU:0, one launch (start us, length us, event | category | flops | bytes accessed | tf_op | source)
XLA Modules:
  0.0 186.0 jit_solution(4023462735983177383)
XLA Ops:
  0.0 0.7 convert_bitcast_fusion
  0.7 1.3 pad_maximum_fusion.rt_ref
  2.0 181.2 %shard_map.64 = bf16[384,2048]{1,0:T(8,128)(2,1)} custom-call(f32[16,384]{1,0:T(8,128)} %pad_maximum_fusion.rt_ref, bf16[384,2048]{1,0:T(8,128)(2,1)} %x_hbm.1, bf16[16,2048,512]{2,1,0:T(8,128)(2,1)} %wg_hbm.1, bf16[16,2048,512]{2,1,0:T(8,128)(2,1)} %wu_hbm.1, bf16[16,512,2048]{2,1,0:T(8,128)(2,1)} %wd_hbm.1), custom_call_target="tpu_custom_call" | custom-call | tf_op jit(solution)/shard_map/pallas_call | solution.py:434
  183.2 2.7 %copy.8 = bf16[384,2048]{1,0:T(8,128)(2,1)} copy(bf16[384,2048]{1,0:T(8,128)(2,1)} %shard_map.64) | data formatting | bytes 3145728

commit v4 on v3

v4 whole, which is shorter than its diff:
```python
import functools

import jax
import jax.numpy as jnp
from jax import lax
from jax.experimental import pallas as pl
from jax.experimental.pallas import tpu as pltpu
from jax.sharding import PartitionSpec as P

MESH = pl.DeviceIdType.MESH
ROWS = 384
HALF = 192
PIECE = 96
CAP = 48
DM = 2048
FF = 512
EL = 16
CH = 256
NCH = DM // CH
UNITS = 2 * NCH
WSLOTS = 3
SLOTS = 4


def moe_kernel(ids_ref, gate_ref, x_hbm, wg_hbm, wu_hbm, wd_hbm, y_hbm,
               xa, rtb, key, dt, gp, utri, xdp, hb, wgv, wuv, wdv, ob,
               pm, ps, dr, rf, rs, yst,
               sem_x, sem_w, sem_wd, sem_rs, sem_rr, sem_os, sem_or,
               sem_as, sem_ar, sem_ds, sem_dr, sem_ps, sem_pr, sem_fs, sem_fr,
               sem_ss, sem_sr, sem_ys, sem_yr, sem_yl):
    ep = lax.axis_index('ep')
    ty = lax.axis_index('tp')
    cx = ep // 2
    c = ep % 2
    rF = 1 + c
    rS = 2 - c
    my_rows = pl.ds(pl.multiple_of(c * HALF, HALF), HALF)
    other_rows = pl.ds(pl.multiple_of((1 - c) * HALF, HALF), HALF)

    def dev(r, flip):
        nx = 1 - cx if r & 1 else cx
        nc = 1 - c if flip else c
        ny = 1 - ty if r & 2 else ty
        return {'ep': nx * 2 + nc, 'tp': ny}

    partner = dev(0, True)
    dev_f = {'ep': (cx * c + (1 - cx) * (1 - c)) * 2 + c, 'tp': ty * (1 - c) + (1 - ty) * c}
    dev_s = {'ep': (cx * (1 - c) + (1 - cx) * c) * 2 + c, 'tp': ty * c + (1 - ty) * (1 - c)}

    def rcopy(src, dst, ssem, rsem, device):
        return pltpu.make_async_remote_copy(src_ref=src, dst_ref=dst, send_sem=ssem, recv_sem=rsem,
                                            device_id=device, device_id_type=MESH)

    def w_copies(g):
        e = g % EL
        s = g % WSLOTS
        return (pltpu.make_async_copy(wg_hbm.at[e], wgv.at[s], sem_w.at[s, 0]),
                pltpu.make_async_copy(wu_hbm.at[e], wuv.at[s], sem_w.at[s, 1]))

    def wd_copy(u):
        col = pl.ds(pl.multiple_of((u % NCH) * CH, CH), CH)
        return pltpu.make_async_copy(wd_hbm.at[:, :, col], wdv.at[u % 2], sem_wd.at[u % 2])

    def piece(q):
        return pl.ds(pl.multiple_of(c * HALF + q * PIECE, PIECE), PIECE)

    def c_f(p, q):
        return rcopy(xa.at[p, 0, piece(q)], xa.at[p, rF, piece(q)], sem_as.at[p, 0, q], sem_ar.at[p, 0, q], dev_f)

    def c_s(p, q):
        return rcopy(xa.at[p, 0, piece(q)], xa.at[p, rS, piece(q)], sem_as.at[p, 1, q], sem_ar.at[p, 1, q], dev_s)

    def c_d(p, q):
        return rcopy(xa.at[p, rF, piece(q)], xa.at[p, 3, piece(q)], sem_as.at[p, 2, q], sem_ar.at[p, 2, q], dev_s)

    def c_pair(p, r, q):
        return rcopy(xa.at[p, r, piece(q)], xa.at[p, r, piece(q)], sem_ds.at[p, r, q], sem_dr.at[p, r, q], partner)

    def rows_first(p, q):
        c_f(p, q).wait()
        c_d(p, q).start()
        c_pair(p, rF, q).start()

    def rows_second(p, q):
        c_s(p, q).wait()
        c_pair(p, rS, q).start()

    def rows_third(p, q):
        c_d(p, q).wait()
        c_pair(p, 3, q).start()

    def rows_done(p, r):
        for q in range(2):
            c_pair(p, r, q).wait()

    def own_first(q):
        rows = pl.ds(pl.multiple_of((1 - c) * HALF + q * PIECE, PIECE), PIECE)
        return rcopy(xa.at[c, 0, rows], xa.at[c, 0, rows], sem_os.at[q], sem_or.at[q], partner)

    own_second = rcopy(xa.at[c, 0, my_rows], xa.at[c, 0, my_rows], sem_os.at[2], sem_or.at[2], partner)

    x_load = pltpu.make_async_copy(x_hbm, xa.at[c, 0], sem_x)
    x_load.start()

    rtb[c * 4, 0:8, :] = ids_ref[...].astype(jnp.float32)
    rtb[c * 4, 8:16, :] = gate_ref[...]
    barrier = pltpu.get_barrier_semaphore()
    peers = [(r, flip) for r in range(4) for flip in (False, True) if (r, flip) != (0, False)]
    for r, flip in peers:
        pl.semaphore_signal(barrier, inc=1, device_id=dev(r, flip), device_id_type=MESH)
    pl.semaphore_wait(barrier, len(peers))

    def rt_link(r):
        b = c * 4 + r
        return rcopy(rtb.at[c * 4], rtb.at[b], sem_rs.at[r, 0], sem_rr.at[b], dev(r, False))

    def rt_pair(r):
        b = c * 4 + r
        return rcopy(rtb.at[b], rtb.at[b], sem_rs.at[r, 1], sem_rr.at[b], partner)

    for r in (3, 1, 2):
        rt_link(r).start()
    rt_pair(0).start()
    x_load.wait()
    for q in range(2):
        own_first(q).start()
    for q in range(2):
        @pl.when(c == 1)
        def _():
            own_first(q).wait_recv()

        c_f(0, q).start()
        c_s(0, q).start()
    for q in range(2):
        own_first(q).wait_send()
    own_second.start()
    for g in range(WSLOTS):
        for cp in w_copies(g):
            cp.start()

    t_row = lax.broadcasted_iota(jnp.int32, (ROWS, ROWS), 0)
    t_col = lax.broadcasted_iota(jnp.int32, (ROWS, ROWS), 1)
    utri[...] = jnp.where(t_row < t_col, 1.0, 0.0).astype(jnp.bfloat16)
    for r in (1, 2, 3):
        rt_link(r).wait()
        rt_pair(r).start()
    for r in range(4):
        rt_pair(r).wait_send()
        b = (1 - c) * 4 + r
        pltpu.make_async_copy(rtb.at[b], rtb.at[b], sem_rr.at[b]).wait()

    q_iota = lax.broadcasted_iota(jnp.int32, (CAP, ROWS), 0).astype(jnp.float32)

    def build(b, _):
        p = b // 4
        r = b % 4
        e_iota = (lax.broadcasted_iota(jnp.int32, (EL, ROWS), 0) + ep * EL).astype(jnp.float32)
        chosen = jnp.zeros((EL, ROWS), jnp.float32)
        gate = jnp.zeros((EL, ROWS), jnp.float32)
        for j in range(8):
            hit = rtb[b, j:j + 1, :] == e_iota
            chosen = jnp.where(hit, 1.0, chosen)
            gate = jnp.where(hit, rtb[b, 8 + j:9 + j, :], gate)
        rank = jnp.dot(chosen.astype(jnp.bfloat16), utri[...], preferred_element_type=jnp.float32)
        kk = jnp.where(chosen > 0.0, rank, -1.0)
        key[b] = kk
        hots = []
        for e in range(EL):
            hit = kk[e:e + 1, :] == q_iota
            hots.append(jnp.where(hit, 1.0, 0.0))
            gsum = jnp.sum(jnp.where(hit, gate[e:e + 1, :], 0.0), axis=1, keepdims=True)
            gp[p, e, pl.ds(pl.multiple_of(r * CAP, CAP), CAP), :] = jnp.broadcast_to(gsum, (CAP, 128))
        dt[b] = jnp.concatenate(hots, axis=0).T.astype(jnp.bfloat16)
        return 0

    lax.fori_loop(0, 8, build, 0)

    own_second.wait()

    @pl.when(c == 0)
    def _():
        for q in range(2):
            own_first(q).wait_recv()

    def dispatch_group(r, eg, put):
        kk = key.at[r]
        hots = [jnp.where(kk[pl.ds(eg * 4 + j, 1), :] == q_iota, 1.0, 0.0) for j in range(4)]
        hot = jnp.concatenate(hots, axis=0).astype(jnp.bfloat16)
        for n in range(4):
            res = jnp.dot(hot, xa[0, r, :, n * 512:(n + 1) * 512],
                          preferred_element_type=jnp.float32).astype(jnp.bfloat16)
            for j in range(4):
                for m in range(2):
                    put(j, n * 2 + m, r, res[j * CAP:(j + 1) * CAP, m * 256:(m + 1) * 256])

    def put_wdv(eg):
        def put(j, q, r, val):
            rows = pl.ds(pl.multiple_of((q % 2) * HALF + r * CAP, CAP), CAP)
            wdv[eg, j * 4 + q // 2, rows, :] = val
        return put

    def put_ob(j, q, r, val):
        rows = pl.ds(pl.multiple_of((q % 4) * HALF + r * CAP, CAP), CAP)
        ob[j * 2 + q // 4, rows, :] = val

    def put_xdp(j, q, r, val):
        xdp[j, pl.ds(pl.multiple_of(r * CAP, CAP), CAP), q * 256:(q + 1) * 256] = val

    def dispatch_block(r, _):
        @pl.when(r == 1)
        def _():
            rows_first(0, 0)
            rows_second(0, 0)
            rows_first(0, 1)
            c_s(1, 0).start()
            c_s(1, 1).start()
            rows_second(0, 1)
            rows_done(0, 1)
            rows_done(0, 2)

        for eg in range(2):
            dispatch_group(r, eg, put_wdv(eg))
        dispatch_group(r, 2, put_ob)
        dispatch_group(r, 3, put_xdp)
        return 0

    lax.fori_loop(0, 3, dispatch_block, 0)
    rows_third(0, 0)
    rows_third(0, 1)
    c_f(1, 0).start()
    c_f(1, 1).start()
    rows_done(0, 3)

    def expert(p, e, rows_of):
        g = p * EL + e
        for cp in w_copies(g):
            cp.wait()
        s = g % WSLOTS
        xe = rows_of()
        for n in range(2):
            cols = slice(n * 256, (n + 1) * 256)
            a = jnp.dot(xe, wgv[s, :, cols], preferred_element_type=jnp.float32)
            b = jnp.dot(xe, wuv[s, :, cols], preferred_element_type=jnp.float32)
            hb[p, e, :, cols] = (a * jax.nn.sigmoid(a) * b).astype(jnp.bfloat16)

        @pl.when(e + WSLOTS < EL)
        def _():
            for cp in w_copies(g + WSLOTS):
                cp.start()

    def dispatch(p, quad, blocks):
        for r in blocks:
            hots = [jnp.where(key[p * 4 + r, pl.ds(4 * quad + j, 1), :] == q_iota, 1.0, 0.0) for j in range(4)]
            hot = jnp.concatenate(hots, axis=0).astype(jnp.bfloat16)
            for n in range(4):
                cols = slice(n * 512, (n + 1) * 512)
                res = jnp.dot(hot, xa[p, r, :, cols], preferred_element_type=jnp.float32).astype(jnp.bfloat16)
                for j in range(4):
                    xdp[j, r * CAP:(r + 1) * CAP, cols] = res[j * CAP:(j + 1) * CAP]

    def group_wdv(eg, _):
        dispatch_group(3, eg, put_wdv(eg))

        def one(j, _):
            def rows_of():
                return jnp.concatenate([wdv[eg, j * 4 + q // 2, (q % 2) * HALF:(q % 2 + 1) * HALF, :]
                                        for q in range(8)], axis=1)
            expert(0, eg * 4 + j, rows_of)

            @pl.when((eg == 1) & (j == 1))
            def _():
                rows_first(1, 0)
                rows_second(1, 0)
            return 0

        lax.fori_loop(0, 4, one, 0)
        return 0

    def experts_ob(j, _):
        def rows_of():
            return jnp.concatenate([ob[j * 2 + q // 4, (q % 4) * HALF:(q % 4 + 1) * HALF, :]
                                    for q in range(8)], axis=1)
        expert(0, 8 + j, rows_of)
        return 0

    def experts_xdp(j, _):
        expert(0, 12 + j, lambda: xdp[j])

        @pl.when(j == 0)
        def _():
            rows_first(1, 1)
            rows_second(1, 1)
        return 0

    lax.fori_loop(0, 2, group_wdv, 0)
    wd_copy(0).start()
    dispatch_group(3, 2, put_ob)
    lax.fori_loop(0, 4, experts_ob, 0)
    dispatch_group(3, 3, put_xdp)
    lax.fori_loop(0, 4, experts_xdp, 0)
    for g in range(WSLOTS):
        if g == 2:
            wd_copy(1).start()
        for cp in w_copies(EL + g):
            cp.start()

    def k_pair(u):
        s = u % 2
        return rcopy(ps, dr.at[s], sem_ps, sem_pr.at[s], partner)

    def k_first(u, which):
        s = u % SLOTS
        src = pm.at[s, 3] if which == 0 else pm.at[s, rF]
        return rcopy(src, rf.at[s, which], sem_fs.at[s, which], sem_fr.at[s, which], dev_f)

    def k_second(u):
        s = u % SLOTS
        return rcopy(pm.at[s, rS], rs.at[s], sem_ss.at[s], sem_sr.at[s], dev_s)

    def k_out(u):
        k = u % NCH
        cols = pl.ds(pl.multiple_of(k * CH, CH), CH)
        return rcopy(yst.at[u % SLOTS], y_hbm.at[my_rows, cols], sem_ys.at[k], sem_yr.at[k], partner)

    def k_local(u):
        k = u % NCH
        cols = pl.ds(pl.multiple_of(k * CH, CH), CH)
        return pltpu.make_async_copy(yst.at[u % SLOTS], y_hbm.at[my_rows, cols], sem_yl.at[k])

    def out_drain(u):
        @pl.when(c == u // NCH)
        def _():
            k_local(u).wait()

        @pl.when(c != u // NCH)
        def _():
            k_out(u).wait_send()

    def stage1(u):
        k_pair(u).wait()
        s = u % SLOTS
        for r in (3, 1, 2, 0):
            pm[s, r] = pm[s, r] + dr[u % 2, r]
        k_first(u, 0).start()
        k_first(u, 1).start()

    def stage2(u):
        s = u % SLOTS
        k_first(u, 0).wait()
        pm[s, rS] = pm[s, rS] + rf[s, 0]
        k_second(u).start()
        k_first(u, 1).wait()
        pm[s, 0] = pm[s, 0] + rf[s, 1]

    def stage3(u):
        s = u % SLOTS
        k_second(u).wait()

        @pl.when(u >= SLOTS)
        def _():
            out_drain(u - SLOTS)

        yst[s] = (pm[s, 0] + rs[s]).astype(jnp.bfloat16)

        @pl.when(c == u // NCH)
        def _():
            k_local(u).start()

        @pl.when(c != u // NCH)
        def _():
            k_out(u).start()

    def compute(u):
        p = u // NCH
        s2 = u % 2
        s4 = u % SLOTS
        wd_copy(u).wait()

        for e in range(EL):
            o = jnp.dot(hb[p, e], wdv[s2, e], preferred_element_type=jnp.float32)
            g = gp[p, e]
            o = o * jnp.concatenate([g, g], axis=1)
            hi = o.astype(jnp.bfloat16)
            rest = o - hi.astype(jnp.float32)
            mid = rest.astype(jnp.bfloat16)
            lo = (rest - mid.astype(jnp.float32)).astype(jnp.bfloat16)
            rows = slice(e * CAP, (e + 1) * CAP)
            for r in range(4):
                part = slice(r * CAP, (r + 1) * CAP)
                ob[r, rows, :] = hi[part]
                ob[4 + r, rows, :] = mid[part]
                ob[8 + r, rows, :] = lo[part]

        @pl.when(u + 2 < UNITS)
        def _():
            wd_copy(u + 2).start()

        def combine(rows, store):
            for r in range(4):
                sel = dt[p * 4 + r, rows, :]
                acc = jnp.dot(sel, ob[r], preferred_element_type=jnp.float32)
                acc += jnp.dot(sel, ob[4 + r], preferred_element_type=jnp.float32)
                acc += jnp.dot(sel, ob[8 + r], preferred_element_type=jnp.float32)
                store(r, acc)

        def store_other(r, acc):
            ps[r] = acc

        def store_mine(r, acc):
            pm[s4, r] = acc

        combine(other_rows, store_other)
        k_pair(u).start()
        combine(my_rows, store_mine)

    def unit(i, _):
        @pl.when(i >= 4)
        def _():
            stage3(i - 4)

        @pl.when(i < UNITS)
        def _():
            compute(i)

        def links():
            @pl.when((i >= 2) & (i < UNITS + 2))
            def _():
                stage2(i - 2)

            @pl.when(i < UNITS)
            def _():
                stage1(i)

        @pl.when((i < EL // 2) & (i % 2 == 0))
        def _():
            dispatch(1, i // 2, (0, 1, 2))

        @pl.when(i == 0)
        def _():
            stage1(i)
            rows_third(1, 0)
            rows_third(1, 1)
            rows_done(1, 3)

        @pl.when((i < EL // 2) & (i % 2 == 0))
        def _():
            dispatch(1, i // 2, (3,))

        @pl.when(i < EL // 2)
        def _():
            expert(1, 2 * i, lambda: xdp[(2 * i) % 4])

        @pl.when(i > 0)
        def _():
            links()

        @pl.when(i < EL // 2)
        def _():
            expert(1, 2 * i + 1, lambda: xdp[(2 * i) % 4 + 1])
        return 0

    rows_done(1, 1)
    rows_done(1, 2)
    lax.fori_loop(0, UNITS + 4, unit, 0)

    for u in range(UNITS - SLOTS, UNITS):
        out_drain(u)
    for k in range(NCH):
        k_out(k).wait_recv()


def solution(mesh):
    row_spec = P(('dp', 'ep', 'tp'), None)
    bf, f32 = jnp.bfloat16, jnp.float32

    def local_moe(x, ids, gate, wg, wu, wd):
        anyspec = pl.BlockSpec(memory_space=pl.ANY)
        dma = pltpu.SemaphoreType.DMA
        return pl.pallas_call(
            moe_kernel,
            out_shape=jax.ShapeDtypeStruct((ROWS, DM), bf),
            in_specs=[pl.BlockSpec(memory_space=pltpu.VMEM)] * 2 + [anyspec] * 4,
            out_specs=anyspec,
            scratch_shapes=[
                pltpu.VMEM((2, 4, ROWS, DM), bf),
                pltpu.VMEM((8, 16, ROWS), f32),
                pltpu.VMEM((8, EL, ROWS), f32),
                pltpu.VMEM((8, ROWS, EL * CAP), bf),
                pltpu.VMEM((2, EL, 4 * CAP, 128), f32),
                pltpu.VMEM((ROWS, ROWS), bf),
                pltpu.VMEM((4, 4 * CAP, DM), bf),
                pltpu.VMEM((2, EL, 4 * CAP, FF), bf),
                pltpu.VMEM((WSLOTS, DM, FF), bf),
                pltpu.VMEM((WSLOTS, DM, FF), bf),
                pltpu.VMEM((2, EL, FF, CH), bf),
                pltpu.VMEM((12, EL * CAP, CH), bf),
                pltpu.VMEM((SLOTS, 4, HALF, CH), f32),
                pltpu.VMEM((4, HALF, CH), f32),
                pltpu.VMEM((2, 4, HALF, CH), f32),
                pltpu.VMEM((SLOTS, 2, HALF, CH), f32),
                pltpu.VMEM((SLOTS, HALF, CH), f32),
                pltpu.VMEM((SLOTS, HALF, CH), bf),
                dma, dma((WSLOTS, 2)), dma((2,)), dma((4, 2)), dma((8,)), dma((3,)), dma((3,)),
                dma((2, 3, 2)), dma((2, 3, 2)), dma((2, 4, 2)), dma((2, 4, 2)), dma, dma((2,)),
                dma((SLOTS, 2)), dma((SLOTS, 2)), dma((SLOTS,)), dma((SLOTS,)), dma((NCH,)), dma((NCH,)), dma((NCH,)),
            ],
            compiler_params=pltpu.CompilerParams(
                collective_id=0, has_side_effects=True, vmem_limit_bytes=67_043_328),
        )(ids.T, gate.T, x, wg, wu, wd)

    return jax.shard_map(
        local_moe, mesh=mesh,
        in_specs=(row_spec, row_spec, row_spec, P('ep', None, 'tp'), P('ep', None, 'tp'), P('ep', 'tp', None)),
        out_specs=row_spec, check_vma=False)
```

time: 186 us -> 178 us (0.957)
  Pallas kernels: 181 us -> 175 us
  other arithmetic: 2.02 us -> 0 us
    pallas_call x1, Pallas kernels: 181 us -> 175 us  [local_moe(): pl.pallas_call(moe_kernel, out_shape=jax.ShapeDtypeStruct((ROWS, DM), bf)...]
where the time goes in v4:
time: 178 us
  Pallas kernels  175 us (98%)
  local copies, waits for them, and re-layouts  2.73 us (2%)
    pallas_call x1, Pallas kernels, local_moe(): pl.pallas_call(moe_kernel, out_shape=jax.ShapeDtypeStruct((ROWS, DM), bf)...  175 us

profile of v4, /device:TPU:0, one launch (start us, length us, event | category | flops | bytes accessed | tf_op | source)
XLA Modules:
  0.0 178.0 jit_solution(8669250804261144014)
XLA Ops:
  0.0 175.3 %shard_map.64 = bf16[384,2048]{1,0:T(8,128)(2,1)} custom-call(s32[8,384]{1,0:T(8,128)} %bitcast.2, f32[8,384]{1,0:T(8,128)} %bitcast.3, bf16[384,2048]{1,0:T(8,128)(2,1)} %x_hbm.1, bf16[16,2048,512]{2,1,0:T(8,128)(2,1)} %wg_hbm.1, bf16[16,2048,512]{2,1,0:T(8,128)(2,1)} %wu_hbm.1, bf16[16,512,2048]{2,1,0:T(8,128)(2,1)} %wd_hbm.1), custom_call_target="tpu_custom_call" | custom-call | tf_op jit(solution)/shard_map/pallas_call | solution.py:479
  175.3 2.7 %copy.8 = bf16[384,2048]{1,0:T(8,128)(2,1)} copy(bf16[384,2048]{1,0:T(8,128)(2,1)} %shard_map.64) | data formatting | bytes 3145728

commit v5 on v4

--- a/solution.py
+++ b/solution.py
@@ -395,6 +395,14 @@
         def _():
             wd_copy(u + 2).start()
 
+        @pl.when(u == 1)
+        def _():
+            stage1(0)
+
+        @pl.when(u >= 2)
+        def _():
+            stage2(u - 2)
+
         def combine(rows, store):
             for r in range(4):
                 sel = dt[p * 4 + r, rows, :]
@@ -418,45 +426,51 @@
         def _():
             stage3(i - 4)
 
+        @pl.when(i == NCH)
+        def _():
+            for j in (2, 3):
+                expert(1, EL - 4 + j, lambda: xdp[j])
+
         @pl.when(i < UNITS)
         def _():
             compute(i)
 
-        def links():
-            @pl.when((i >= 2) & (i < UNITS + 2))
-            def _():
-                stage2(i - 2)
-
-            @pl.when(i < UNITS)
-            def _():
-                stage1(i)
-
-        @pl.when((i < EL // 2) & (i % 2 == 0))
-        def _():
-            dispatch(1, i // 2, (0, 1, 2))
-
-        @pl.when(i == 0)
-        def _():
-            stage1(i)
+        first = 2 * (i - 1)
+        beside = (i >= 1) & (i < NCH)
+
+        @pl.when(i == 1)
+        def _():
             rows_third(1, 0)
             rows_third(1, 1)
+
+        @pl.when(beside & (i % 2 == 1))
+        def _():
+            dispatch(1, i // 2, (0, 1, 2))
+            stage1(i)
+
+        @pl.when(i == 1)
+        def _():
             rows_done(1, 3)
 
-        @pl.when((i < EL // 2) & (i % 2 == 0))
+        @pl.when(beside & (i % 2 == 1))
         def _():
             dispatch(1, i // 2, (3,))
 
-        @pl.when(i < EL // 2)
-        def _():
-            expert(1, 2 * i, lambda: xdp[(2 * i) % 4])
-
-        @pl.when(i > 0)
-        def _():
-            links()
-
-        @pl.when(i < EL // 2)
-        def _():
-            expert(1, 2 * i + 1, lambda: xdp[(2 * i) % 4 + 1])
+        @pl.when(beside)
+        def _():
+            expert(1, first, lambda: xdp[first % 4])
+
+        @pl.when((i >= UNITS) & (i < UNITS + 2))
+        def _():
+            stage2(i - 2)
+
+        @pl.when((i < UNITS) & (i > 0) & ((i >= NCH) | (i % 2 == 0)))
+        def _():
+            stage1(i)
+
+        @pl.when(beside)
+        def _():
+            expert(1, first + 1, lambda: xdp[first % 4 + 1])
         return 0
 
     rows_done(1, 1)

time: 178 us -> 177 us (level)
  no operation moved by 1% of the time
where the time goes in v5:
time: 177 us; the launch traced here: 176 us
  Pallas kernels  174 us (98%)
  local copies, waits for them, and re-layouts  2.73 us (2%)
    pallas_call x1, Pallas kernels, local_moe(): pl.pallas_call(moe_kernel, out_shape=jax.ShapeDtypeStruct((ROWS, DM), bf)...  174 us

profile of v5, /device:TPU:0, one launch (start us, length us, event | category | flops | bytes accessed | tf_op | source)
XLA Modules:
  0.0 176.4 jit_solution(17917722133810214571)
XLA Ops:
  0.0 173.6 %shard_map.64 = bf16[384,2048]{1,0:T(8,128)(2,1)} custom-call(s32[8,384]{1,0:T(8,128)} %bitcast.2, f32[8,384]{1,0:T(8,128)} %bitcast.3, bf16[384,2048]{1,0:T(8,128)(2,1)} %x_hbm.1, bf16[16,2048,512]{2,1,0:T(8,128)(2,1)} %wg_hbm.1, bf16[16,2048,512]{2,1,0:T(8,128)(2,1)} %wu_hbm.1, bf16[16,512,2048]{2,1,0:T(8,128)(2,1)} %wd_hbm.1), custom_call_target="tpu_custom_call" | custom-call | tf_op jit(solution)/shard_map/pallas_call | solution.py:493
  173.6 2.7 %copy.8 = bf16[384,2048]{1,0:T(8,128)(2,1)} copy(bf16[384,2048]{1,0:T(8,128)(2,1)} %shard_map.64) | data formatting | bytes 3145728

commit v6 on v5

--- a/solution.py
+++ b/solution.py
@@ -339,10 +339,12 @@
     def stage1(u):
         k_pair(u).wait()
         s = u % SLOTS
-        for r in (3, 1, 2, 0):
-            pm[s, r] = pm[s, r] + dr[u % 2, r]
+        pm[s, 3] = pm[s, 3] + dr[u % 2, 3]
         k_first(u, 0).start()
+        pm[s, rF] = pm[s, rF] + dr[u % 2, rF]
         k_first(u, 1).start()
+        pm[s, rS] = pm[s, rS] + dr[u % 2, rS]
+        pm[s, 0] = pm[s, 0] + dr[u % 2, 0]
 
     def stage2(u):
         s = u % SLOTS
@@ -399,10 +401,6 @@
         def _():
             stage1(0)
 
-        @pl.when(u >= 2)
-        def _():
-            stage2(u - 2)
-
         def combine(rows, store):
             for r in range(4):
                 sel = dt[p * 4 + r, rows, :]
@@ -419,6 +417,11 @@
 
         combine(other_rows, store_other)
         k_pair(u).start()
+
+        @pl.when(u >= 2)
+        def _():
+            stage2(u - 2)
+
         combine(my_rows, store_mine)
 
     def unit(i, _):

time: 177 us -> 176 us (level)
  no operation moved by 1% of the time
where the time goes in v6:
time: 176 us
  Pallas kernels  173 us (98%)
  local copies, waits for them, and re-layouts  2.73 us (2%)
    pallas_call x1, Pallas kernels, local_moe(): pl.pallas_call(moe_kernel, out_shape=jax.ShapeDtypeStruct((ROWS, DM), bf)...  173 us

profile of v6, /device:TPU:0, one launch (start us, length us, event | category | flops | bytes accessed | tf_op | source)
XLA Modules:
  0.0 175.9 jit_solution(14629133882702063232)
XLA Ops:
  0.0 173.1 %shard_map.64 = bf16[384,2048]{1,0:T(8,128)(2,1)} custom-call(s32[8,384]{1,0:T(8,128)} %bitcast.2, f32[8,384]{1,0:T(8,128)} %bitcast.3, bf16[384,2048]{1,0:T(8,128)(2,1)} %x_hbm.1, bf16[16,2048,512]{2,1,0:T(8,128)(2,1)} %wg_hbm.1, bf16[16,2048,512]{2,1,0:T(8,128)(2,1)} %wu_hbm.1, bf16[16,512,2048]{2,1,0:T(8,128)(2,1)} %wd_hbm.1), custom_call_target="tpu_custom_call" | custom-call | tf_op jit(solution)/shard_map/pallas_call | solution.py:496
  173.1 2.7 %copy.8 = bf16[384,2048]{1,0:T(8,128)(2,1)} copy(bf16[384,2048]{1,0:T(8,128)(2,1)} %shard_map.64) | data formatting | bytes 3145728
